TPU v7x, 32 devices: a whole 2x2x4 slice. The times are simulated.
32 devices in a mesh: row: 8 (over z, x), col: 2 (over y), depth: 2 (over core).
Axes of the slice: x: 2, y: 2, z: 4, core: 2. Of those that a mesh axis runs over, the one named last changes fastest.
Arguments:
- tokens: bfloat16 [1024, 5376], P('row', 'depth'), may hold values from -6 to 6
- gate_weight: bfloat16 [9216, 5376], P(('col', 'row'), 'depth'), may hold values from -0.078125 to 0.078125
- up_weight: bfloat16 [9216, 5376], P(('col', 'row'), 'depth'), may hold values from -0.078125 to 0.078125
- down_weight: bfloat16 [9216, 5376], P(('col', 'depth'), 'row'), may hold values from -0.09375 to 0.09375
Outputs:
- output: bfloat16 [1024, 5376], P('row', ('col', 'depth'))
All inputs are finite; a program needn't handle non-finite values.
Results may differ from a plain program's by a relative error of at most 0.0049.
Values may be sent and summed in bfloat16 or wider, within the bound.
A program may use at most 128 MiB of HBM per device.

v0:
```python
import jax
import jax.numpy as jnp
from jax import lax
from jax.sharding import PartitionSpec as P


def local(tokens, gate_weight, up_weight, down_weight):
    paired = jnp.stack([gate_weight, up_weight])
    every_token = jnp.einsum(
        "td,gfd->gtf",
        lax.all_gather(tokens, "row", axis=0, tiled=True),
        paired,
        preferred_element_type=jnp.float32,
    )
    partial_sums = lax.all_to_all(every_token, "row", split_axis=1, concat_axis=2, tiled=True)
    share_width = partial_sums.shape[2] // lax.axis_size("depth")
    summed = lax.psum(partial_sums, "depth")
    shares = lax.dynamic_slice_in_dim(summed, lax.axis_index("depth") * share_width, share_width, 2)
    hidden = (jax.nn.silu(shares[0]) * shares[1]).astype(jnp.bfloat16)
    down_terms = jnp.dot(
        hidden,
        lax.all_gather(down_weight, "row", axis=1, tiled=True),
        preferred_element_type=jnp.float32,
    )
    return lax.psum_scatter(down_terms, ("col", "depth"), scatter_dimension=1, tiled=True).astype(
        jnp.bfloat16
    )


def solution(mesh):
    in_specs = (
        P("row", "depth"),
        P(("col", "row"), "depth"),
        P(("col", "row"), "depth"),
        P(("col", "depth"), "row"),
    )
    out_specs = P("row", ("col", "depth"))
    return jax.shard_map(local, mesh=mesh, in_specs=in_specs, out_specs=out_specs, check_vma=False)
```

profile of v0, /device:TPU:0, one launch (start us, length us, event | category | flops | bytes accessed | tf_op | source)
XLA Modules:
  0.0 810.8 jit_solution(2922904456121408201)
XLA Ops:
  6.5 0.0 all-gather.3.cloned.1.call-start
  6.5 0.7 all-gather.3.cloned.1.call-update
  7.3 0.0 all-reduce.2.cloned.1.call-start
  7.3 94.1 %all-gather.3.cloned.1.call-done = bf16[1024,2688]{1,0:T(8,128)(2,1)} async-done(((bf16[128,2688]{1,0:T(8,128)(2,1)}), bf16[1024,2688]{1,0:T(8,128)(2,1)}) %all-gather.3.cloned.1.call-update) | async-done | bytes 5505040 | tf_op jit(solution)/shard_map/all_gather | solution.py:11
  101.4 12.0 %fusion.5 = f32[2,1024,576]{1,2,0:T(8,128)} fusion(bf16[1024,2688]{1,0:T(8,128)(2,1)} %all-gather.3.cloned.1.call-done, bf16[1,576,2688]{2,1,0:T(8,128)(2,1)} %bitcast.29, bf16[1,576,2688]{2,1,0:T(8,128)(2,1)} %bitcast.30), kind=kOutput, calls=%fused_computation.5 | convolution fusion | flops 6344884224 | bytes 16416768 | tf_op jit(solution)/shard_map/td,gfd->gtf/dot_general | solution.py:9
  113.4 8.8 %copy.7 = f32[2,1024,576]{2,0,1:T(2,128)} copy(f32[2,1024,576]{1,2,0:T(8,128)} %fusion.5) | data formatting | bytes 9437184 | tf_op jit(solution)/shard_map/td,gfd->gtf/transpose | solution.py:9
  122.1 118.9 %all_to_all.18 = f32[2,1024,576]{2,0,1:T(2,128)} all-to-all(f32[2,1024,576]{2,0,1:T(2,128)} %copy.7), channel_id=1, replica_groups=mesh['row'=8,'col'=2,'depth'=2] {'row'}, dimensions={1} | all-to-all | bytes 9437184 | tf_op jit(solution)/shard_map/all_to_all | solution.py:15
  241.1 8.7 %copy.11 = f32[2,8,128,576]{2,3,1,0:T(8,128)} copy(f32[2,8,128,576]{3,0,2,1:T(2,128)} %bitcast.27) | data formatting | bytes 9437184 | tf_op jit(solution)/shard_map/all_to_all | solution.py:15
  249.7 0.0 all-reduce.2.cloned.1.call-update
  249.8 0.0 all-gather.5.cloned.1.call-start
  249.8 0.7 all-gather.5.cloned.1.call-update
  250.5 0.0 reduce-scatter.2.cloned.1.call-start
  250.6 27.2 %all-reduce.2.cloned.1.call-done = f32[2,128,4608]{1,2,0:T(8,128)} async-done(((f32[2,128,4608]{1,2,0:T(8,128)}), f32[2,128,4608]{1,2,0:T(8,128)}) %all-reduce.2.cloned.1.call-update) | async-done | bytes 4718608 | tf_op jit(solution)/shard_map/psum | solution.py:17
  277.8 475.7 %all-gather.5.cloned.1.call-done = bf16[2304,5376]{0,1:T(8,128)(2,1)} async-done(((bf16[2304,672]{0,1:T(8,128)(2,1)}), bf16[2304,5376]{0,1:T(8,128)(2,1)}) %all-gather.5.cloned.1.call-update) | async-done | bytes 24772624 | tf_op jit(solution)/shard_map/all_gather | solution.py:22
  753.5 13.3 %fusion.12 = f32[128,5376]{0,1:T(8,128)} fusion(bf16[2304,5376]{0,1:T(8,128)(2,1)} %all-gather.5.cloned.1.call-done, f32[2,128,4608]{1,2,0:T(8,128)} %all-reduce.2.cloned.1.call-done, s32[]{:T(128)S(6)} %add.13, s32[]{:T(128)S(6)} %select_n.3), kind=kOutput, calls=%fused_computation.10 | convolution fusion | flops 3172663296 | bytes 29884424 | tf_op jit(solution)/shard_map/dot_general | solution.py:20
  766.9 0.0 reduce-scatter.2.cloned.1.call-update
  766.9 35.5 %reduce-scatter.2.cloned.1.call-done = f32[128,1344]{0,1:T(8,128)} async-done(((f32[128,5376]{0,1:T(8,128)}), f32[128,1344]{0,1:T(8,128)}) %reduce-scatter.2.cloned.1.call-update) | async-done | bytes 688144 | tf_op jit(solution)/shard_map/reduce_scatter | solution.py:25
  802.4 1.9 convert_element_type.7
Async XLA Ops:
  6.5 94.9 %all-gather.3.cloned.1.call-start = ((), (), s32[]{:S(2)}) async-start(), calls=%async_computation.2 | async-start | bytes 6193152 | tf_op jit(solution)/shard_map/all_gather | solution.py:11
  7.3 270.5 %all-reduce.2.cloned.1.call-start = ((), (), s32[]{:S(2)}) async-start(), calls=%async_computation.3 | async-start | bytes 9437184 | tf_op jit(solution)/shard_map/psum | solution.py:17
  249.8 503.8 %all-gather.5.cloned.1.call-start = ((), (), s32[]{:S(2)}) async-start(), calls=%async_computation.4 | async-start | bytes 27869184 | tf_op jit(solution)/shard_map/all_gather | solution.py:22
  250.5 551.9 %reduce-scatter.2.cloned.1.call-start = ((), (), s32[]{:S(2)}) async-start(), calls=%async_computation.5 | async-start | bytes 3440640 | tf_op jit(solution)/shard_map/reduce_scatter | solution.py:25
Sparse Core Ops, SparseCore 0:
  9.5 91.8 all-gather.2
  249.9 27.8 all-reduce.1
  279.3 474.1 all-gather.4
  767.0 35.2 reduce-scatter.1
where the time goes:
time: 811 us
  waiting for transfers between devices  634 us (78%)
  blocking collectives  119 us (15%)
  matrix products  25.3 us (3%)
  local copies, waits for them, and re-layouts  17.5 us (2%)
  between operations  13.1 us (2%)
    all_gather x1, waiting for transfers between devices, local(): lax.all_gather(down_weight, 'row', axis=1, tiled=True)  476 us
    all_to_all x1, blocking collectives, local(): lax.all_to_all(every_token, 'row', split_axis=1, concat_axis=2, tiled=True)  119 us
    all_gather x1, waiting for transfers between devices, local(): lax.all_gather(tokens, 'row', axis=0, tiled=True)  94.1 us
    reduce_scatter x1, waiting for transfers between devices, local(): lax.psum_scatter(down_terms, ('col', 'depth'), scatter_dimension=1, tiled...  35.5 us
    psum x1, waiting for transfers between devices, local(): summed = lax.psum(partial_sums, 'depth')  27.2 us
  transfers between devices with their start and end apart: 4, of which 4 were waited for; matrix products, arithmetic and copies ran while one was open for 0% of the time, Pallas kernels for 0%

commit v1 on v0

--- a/solution.py
+++ b/solution.py
@@ -17,11 +17,8 @@
     summed = lax.psum(partial_sums, "depth")
     shares = lax.dynamic_slice_in_dim(summed, lax.axis_index("depth") * share_width, share_width, 2)
     hidden = (jax.nn.silu(shares[0]) * shares[1]).astype(jnp.bfloat16)
-    down_terms = jnp.dot(
-        hidden,
-        lax.all_gather(down_weight, "row", axis=1, tiled=True),
-        preferred_element_type=jnp.float32,
-    )
+    _keep_up_boxes = lambda packet: jnp.concatenate(lax.all_gather(packet, "row"), axis=1)
+    down_terms = jnp.dot(hidden, _keep_up_boxes(down_weight), preferred_element_type=jnp.float32)
     return lax.psum_scatter(down_terms, ("col", "depth"), scatter_dimension=1, tiled=True).astype(
         jnp.bfloat16
     )

time: 811 us -> 721 us (0.89)
  waiting for transfers between devices: 634 us -> 450 us
  blocking collectives: 119 us -> 183 us
  local copies, waits for them, and re-layouts: 17.5 us -> 46.2 us
    all_gather x1, waiting for transfers between devices: 476 us -> 316 us  [local(): lax.all_gather(packet, 'row')]
    all_to_all x1, blocking collectives: 119 us -> 183 us  [local(): lax.all_to_all(every_token, 'row', split_axis=1, concat_axis=2, tiled=True)]
    psum x1, waiting for transfers between devices: 27.2 us -> 2.6 us  [local(): summed = lax.psum(partial_sums, 'depth')]
    unnamed x0 -> x1, local copies, waits for them, and re-layouts: none -> 16.8 us
    reshape x0 -> x1, local copies, waits for them, and re-layouts: none -> 12.1 us  [local(): jnp.concatenate(lax.all_gather(packet, 'row'), axis=1)]
  transfers between devices with their start and end apart: 4 -> 4, of which waited for: 4 -> 4; matrix products, arithmetic and copies ran while one was open for 0% -> 8% of each run, Pallas kernels for 0% -> 0%
where the time goes in v1:
time: 721 us; the launch traced here: 720 us
  waiting for transfers between devices  450 us (62%)
  blocking collectives  183 us (25%)
  local copies, waits for them, and re-layouts  46.2 us (6%)
  matrix products  25.3 us (4%)
  between operations  13.1 us (2%)
    all_gather x1, waiting for transfers between devices, local(): lax.all_gather(packet, 'row')  316 us
    all_to_all x1, blocking collectives, local(): lax.all_to_all(every_token, 'row', split_axis=1, concat_axis=2, tiled=True)  183 us
    all_gather x1, waiting for transfers between devices, local(): lax.all_gather(tokens, 'row', axis=0, tiled=True)  93.3 us
    reduce_scatter x1, waiting for transfers between devices, local(): lax.psum_scatter(down_terms, ('col', 'depth'), scatter_dimension=1, tiled...  36.7 us
    unnamed x1, local copies, waits for them, and re-layouts  16.8 us
  transfers between devices with their start and end apart: 4, of which 4 were waited for; matrix products, arithmetic and copies ran while one was open for 8% of the time, Pallas kernels for 0%

profile of v1, /device:TPU:0, one launch (start us, length us, event | category | flops | bytes accessed | tf_op | source)
XLA Modules:
  0.0 720.1 jit_solution(5834530495781599081)
XLA Ops:
  6.5 0.0 all-gather.4.cloned.1.call-start
  6.5 0.7 all-gather.4.cloned.1.call-update
  7.3 0.0 all-gather.6.cloned.1.call-start
  7.3 0.7 all-gather.6.cloned.1.call-update
  8.0 0.0 all-reduce.2.cloned.1.call-start
  8.1 93.3 %all-gather.4.cloned.1.call-done = bf16[1024,2688]{1,0:T(8,128)(2,1)} async-done(((bf16[128,2688]{1,0:T(8,128)(2,1)}), bf16[1024,2688]{1,0:T(8,128)(2,1)}) %all-gather.4.cloned.1.call-update) | async-done | bytes 5505040 | tf_op jit(solution)/shard_map/all_gather | solution.py:11
  101.4 12.0 %fusion.5 = f32[2,1024,576]{1,2,0:T(8,128)} fusion(bf16[1024,2688]{1,0:T(8,128)(2,1)} %all-gather.4.cloned.1.call-done, bf16[1,576,2688]{2,1,0:T(8,128)(2,1)} %bitcast.30, bf16[1,576,2688]{2,1,0:T(8,128)(2,1)} %bitcast.31), kind=kOutput, calls=%fused_computation.5 | convolution fusion | flops 6344884224 | bytes 16416768 | tf_op jit(solution)/shard_map/td,gfd->gtf/dot_general | solution.py:9
  113.4 8.7 %copy.10 = f32[2,1024,576]{2,0,1:T(2,128)} copy(f32[2,1024,576]{1,2,0:T(8,128)} %fusion.5) | data formatting | bytes 9437184 | tf_op jit(solution)/shard_map/td,gfd->gtf/transpose | solution.py:9
  122.1 183.3 %all_to_all.18 = f32[2,1024,576]{2,0,1:T(2,128)} all-to-all(f32[2,1024,576]{2,0,1:T(2,128)} %copy.10), channel_id=1, replica_groups=mesh['row'=8,'col'=2,'depth'=2] {'row'}, dimensions={1} | all-to-all | bytes 9437184 | tf_op jit(solution)/shard_map/all_to_all | solution.py:15
  305.4 8.7 %copy.15 = f32[2,8,128,576]{2,3,1,0:T(8,128)} copy(f32[2,8,128,576]{3,0,2,1:T(2,128)} %bitcast.28) | data formatting | bytes 9437184 | tf_op jit(solution)/shard_map/all_to_all | solution.py:15
  314.1 0.0 all-reduce.2.cloned.1.call-update
  314.1 0.0 reduce-scatter.2.cloned.1.call-start
  314.2 316.1 %all-gather.6.cloned.1.call-done = bf16[18432,672]{0,1:T(8,128)(2,1)} async-done(((bf16[2304,672]{0,1:T(8,128)(2,1)}), bf16[18432,672]{0,1:T(8,128)(2,1)}) %all-gather.6.cloned.1.call-update) | async-done | bytes 24772624 | tf_op jit(solution)/shard_map/all_gather | solution.py:20
  630.3 16.8 %copy.16 = bf16[84,8,8,2304]{3,2,1,0:T(8,128)(2,1)S(1)} copy(bf16[84,8,8,2304]{3,1,2,0:T(8,128)(2,1)} %bitcast.26) | data formatting | bytes 49545216
  647.0 12.1 %copy.13 = bf16[2304,8,672]{0,2,1:T(8,128)(2,1)} copy(bf16[2304,8,672]{0,1,2:T(8,128)(2,1)S(1)} %bitcast.25) | data formatting | bytes 49545216 | tf_op jit(solution)/shard_map/reshape | solution.py:20
  659.1 2.6 all-reduce.2.cloned.1.call-done
  661.7 13.3 %fusion.11 = f32[128,5376]{0,1:T(8,128)} fusion(bf16[2304,5376]{0,1:T(8,128)(2,1)} %bitcast.27, f32[2,128,4608]{1,2,0:T(8,128)} %all-reduce.2.cloned.1.call-done, s32[]{:T(128)S(6)} %add.14, s32[]{:T(128)S(6)} %select_n.3), kind=kOutput, calls=%fused_computation.8 | convolution fusion | flops 3172663296 | bytes 29884424 | tf_op jit(solution)/shard_map/dot_general | solution.py:21
  675.0 0.0 reduce-scatter.2.cloned.1.call-update
  675.1 36.7 %reduce-scatter.2.cloned.1.call-done = f32[128,1344]{0,1:T(8,128)} async-done(((f32[128,5376]{0,1:T(8,128)}), f32[128,1344]{0,1:T(8,128)}) %reduce-scatter.2.cloned.1.call-update) | async-done | bytes 688144 | tf_op jit(solution)/shard_map/reduce_scatter | solution.py:22
  711.7 1.9 convert_element_type.11
Async XLA Ops:
  6.5 94.9 %all-gather.4.cloned.1.call-start = ((), (), s32[]{:S(2)}) async-start(), calls=%async_computation.2 | async-start | bytes 6193152 | tf_op jit(solution)/shard_map/all_gather | solution.py:11
  7.3 623.0 %all-gather.6.cloned.1.call-start = ((), (), s32[]{:S(2)}) async-start(), calls=%async_computation.5 | async-start | bytes 27869184 | tf_op jit(solution)/shard_map/all_gather | solution.py:20
  8.0 653.7 %all-reduce.2.cloned.1.call-start = ((), (), s32[]{:S(2)}) async-start(), calls=%async_computation.3 | async-start | bytes 9437184 | tf_op jit(solution)/shard_map/psum | solution.py:17
  314.1 397.6 %reduce-scatter.2.cloned.1.call-start = ((), (), s32[]{:S(2)}) async-start(), calls=%async_computation.4 | async-start | bytes 3440640 | tf_op jit(solution)/shard_map/reduce_scatter | solution.py:22
Sparse Core Ops, SparseCore 0:
  9.5 91.8 all-gather.3
  102.9 527.2 all-gather.5
  632.8 28.8 all-reduce.1
  675.2 36.5 reduce-scatter.1
